TPU v7x, 64 devices: a 2x2x8 block of a 4x4x8 slice. The times are simulated.
64 devices in a mesh: dp: 8 (over x, y, core), tp: 8 (over z).
Axes of the slice: x: 2, y: 2, z: 8, core: 2. Of those that a mesh axis runs over, the one named last changes fastest.
The devices are a block of a 4x4x8 slice.
Arguments:
- x: bfloat16 [512, 2048], P('dp'), parts along dimension 0
- k_cache: bfloat16 [512, 1024, 32, 64], P('dp', None, 'tp'), parts along dimension 0
- v_cache: bfloat16 [512, 1024, 32, 64], P('dp', None, 'tp'), parts along dimension 0
- gain_a: bfloat16 [2048], replicated
- wq: bfloat16 [2048, 2048], P(None, 'tp')
- wo: bfloat16 [2048, 2048], P('tp')
- gain_m: bfloat16 [2048], replicated
- w_gate: bfloat16 [2048, 5120], P(None, 'tp')
- w_up: bfloat16 [2048, 5120], P(None, 'tp')
- w_down: bfloat16 [5120, 2048], P('tp')
Outputs:
- output: bfloat16 [512, 2048], P('dp'), parts along dimension 0
There are 8 independent parts. A program takes and returns all parts, laid end to end along the dimension named above; an argument that names none is the same for every part.
All inputs are finite; a program needn't handle non-finite values.
Results may differ from a plain program's by a relative error of at most 0.017.
Values are sent between devices in bfloat16 or wider.
A program may use at most 768 MiB of HBM per device.

v0:
```python
import jax
import jax.numpy as jnp
from jax import lax
from jax.sharding import PartitionSpec as P

HEAD = 64
THETA = 10000


def normed(x, gain):
    wide = x.astype(jnp.float32)
    scale = lax.rsqrt(jnp.mean(wide * wide, -1, keepdims=True) + 1e-6)
    return (wide * scale * gain.astype(jnp.float32)).astype(jnp.bfloat16)


def turned(t, place, theta):
    half = t.shape[-1] // 2
    angle = place.astype(jnp.float32)[:, None] * theta ** (-jnp.arange(half, dtype=jnp.float32) / half)
    cos, sin = jnp.cos(angle)[:, None], jnp.sin(angle)[:, None]
    a, b = t[..., :half].astype(jnp.float32), t[..., half:].astype(jnp.float32)
    return jnp.concatenate([a * cos - b * sin, b * cos + a * sin], -1).astype(jnp.bfloat16)


def matmul(a, w):
    return jnp.dot(a, w, preferred_element_type=jnp.float32).astype(jnp.bfloat16)


def einsum(form, a, b):
    return jnp.einsum(form, a.astype(jnp.float32), b.astype(jnp.float32))


def seen_by(a, wq, k_cache, v_cache, head, theta):
    batch, cache, kv_heads = k_cache.shape[:3]
    place = jnp.full((batch,), cache - 1)
    q = turned(matmul(a, wq).reshape(batch, -1, head), place, theta).reshape(batch, kv_heads, -1, head)
    scores = einsum("bgsd,bugd->bgsu", q, k_cache) * head**-0.5
    weights = jax.nn.softmax(scores, -1).astype(jnp.bfloat16)
    return einsum("bgsu,bugd->bgsd", weights, v_cache).astype(jnp.bfloat16).reshape(batch, -1)


def hidden_of(b, w_gate, w_up):
    gate = jnp.dot(b, w_gate, preferred_element_type=jnp.float32)
    up = jnp.dot(b, w_up, preferred_element_type=jnp.float32)
    return (jax.nn.silu(gate) * up).astype(jnp.bfloat16)


def solution(mesh):
    def added(t, term):
        return (t.astype(jnp.float32) + lax.psum(term.astype(jnp.bfloat16), "tp").astype(jnp.float32)).astype(jnp.bfloat16)

    def step(x, k_cache, v_cache, gain_a, wq, wo, gain_m, w_gate, w_up, w_down):
        seen = seen_by(normed(x, gain_a), wq, k_cache, v_cache, HEAD, THETA)
        h = added(x, jnp.dot(seen, wo, preferred_element_type=jnp.float32))
        return added(h, jnp.dot(hidden_of(normed(h, gain_m), w_gate, w_up), w_down, preferred_element_type=jnp.float32))

    states, cache, columns, rows_of = P("dp", None), P("dp", None, "tp", None), P(None, "tp"), P("tp", None)
    return jax.shard_map(
        step,
        mesh=mesh,
        in_specs=(states, cache, cache, P(None), columns, rows_of, P(None), columns, columns, rows_of),
        out_specs=states,
        check_vma=False,
    )
```

profile of v0, /device:TPU:28, one launch (start us, length us, event | category | flops | bytes accessed | tf_op | source)
XLA Modules:
  0.0 194.2 jit_solution(2473001386020462546)
XLA Ops:
  6.5 0.0 copy-start
  6.6 0.0 all-reduce.3.cloned.1.call-start
  6.6 0.8 convert_element_type.66
  7.5 1.1 fusion.11
  8.6 1.7 convolution_convert_fusion.2
  10.2 0.1 copy.11
  10.4 0.1 fusion.34
  10.5 0.1 copy.12
  10.6 13.8 %fusion.45 = f32[64,4,1,1024]{3,2,1,0:T(1,128)} fusion(bf16[64,4,64,1]{2,3,1,0:T(2,128)(2,1)S(1)} %copy.12, bf16[64,1024,4,64]{1,3,2,0:T(8,128)(2,1)} %param.11), kind=kOutput, calls=%fused_computation.58 | convolution fusion | flops 33554432 | bytes 34635776 | tf_op jit(solution)/shard_map/bgsd,bugd->bgsu/dot_general | solution.py:29
  24.5 2.6 %fusion.6 = bf16[64,4,1024,1]{2,0,1,3:T(8,128)(2,1)S(1)} fusion(f32[64,4,1,1024]{3,2,1,0:T(1,128)} %fusion.45), kind=kOutput, calls=%fused_computation.8 | output fusion | flops 1051134 | bytes 1572864 | tf_op jit(solution)/shard_map/div | solution.py:37
  27.1 0.0 copy-start.2
  27.1 0.0 copy-start.1
  27.1 14.0 %fusion.8 = f32[64,4,1,64]{3,2,1,0:T(1,128)S(1)} fusion(bf16[64,1024,4,64]{1,3,2,0:T(8,128)(2,1)} %param.12, bf16[64,4,1024,1]{2,0,1,3:T(8,128)(2,1)S(1)} %fusion.6), kind=kOutput, calls=%fused_computation.13 | convolution fusion | flops 33554432 | bytes 34144256 | tf_op jit(solution)/shard_map/bgsu,bugd->bgsd/dot_general | solution.py:29
  41.2 0.1 reshape.62
  41.3 2.2 %convolution_convert_fusion.1 = bf16[64,2048]{1,0:T(8,128)(2,1)} fusion(bf16[64,256]{1,0:T(8,128)(2,1)S(1)} %reshape.62, bf16[256,2048]{1,0:T(8,128)(2,1)} %param.15), kind=kOutput, calls=%fused_computation.3 | convolution fusion | flops 67239936 | bytes 1343488 | tf_op jit(solution)/shard_map/dot_general | solution.py:53
  43.5 0.1 all-reduce.3.cloned.1.call-update
  43.6 0.1 all-reduce.5.cloned.1.call-start
  43.6 0.0 copy-done.2
  43.7 70.0 %all-reduce.3.cloned.1.call-done = bf16[64,2048]{1,0:T(8,128)(2,1)} async-done(((bf16[64,2048]{1,0:T(8,128)(2,1)}), bf16[64,2048]{1,0:T(8,128)(2,1)}) %all-reduce.3.cloned.1.call-update) | async-done | bytes 262160 | tf_op jit(solution)/shard_map/psum | solution.py:49
  113.7 0.0 copy-done.1
  113.7 1.1 fusion.15
  114.8 2.4 %fusion.31 = f32[64,640]{1,0:T(8,128)S(1)} fusion(bf16[2048,640]{1,0:T(8,128)(2,1)} %param.17, bf16[64,2048]{1,0:T(8,128)(2,1)S(1)} %get-tuple-element.6, f32[2048]{0:T(1024)S(1)} %convert_element_type.77, f32[64]{0:T(128)S(1)} %add_rsqrt_fusion), kind=kOutput, calls=%fused_computation.43 | convolution fusion | flops 168296448 | bytes 3055872 | tf_op jit(solution)/shard_map/dot_general | solution.py:42
  117.2 0.0 copy-done
  117.2 3.6 %convolution_convert_fusion = bf16[64,2048]{1,0:T(8,128)(2,1)} fusion(bf16[640,2048]{1,0:T(8,128)(2,1)S(1)} %copy-done, bf16[2048,640]{1,0:T(8,128)(2,1)} %param.18, f32[64,640]{1,0:T(8,128)S(1)} %fusion.31, bf16[64,2048]{1,0:T(8,128)(2,1)S(1)} %get-tuple-element.6, f32[2048]{0:T(1024)S(1)} %convert_element_type.77, f32[64]{0:T(128)S(1)} %add_rsqrt_fusion), kind=kOutput, calls=%fused_computation.2 | convolution fusion | flops 336445440 | bytes 5939456 | tf_op jit(solution)/shard_map/dot_general | solution.py:54
  120.8 0.1 all-reduce.5.cloned.1.call-update
  120.8 64.8 %all-reduce.5.cloned.1.call-done = bf16[64,2048]{1,0:T(8,128)(2,1)} async-done(((bf16[64,2048]{1,0:T(8,128)(2,1)}), bf16[64,2048]{1,0:T(8,128)(2,1)}) %all-reduce.5.cloned.1.call-update) | async-done | bytes 262160 | tf_op jit(solution)/shard_map/psum | solution.py:49
  185.6 1.7 fusion.18
  (6 shorter events, 0.1 us)
Async XLA Ops:
  6.5 110.6 %copy-start = (bf16[640,2048]{1,0:T(8,128)(2,1)S(1)}, bf16[640,2048]{1,0:T(8,128)(2,1)}, u32[]{:S(2)}) copy-start(bf16[640,2048]{1,0:T(8,128)(2,1)} %param.19) | copy-start | bytes 7864324
  6.6 107.1 %all-reduce.3.cloned.1.call-start = ((), (), s32[]{:S(2)}) async-start(), calls=%async_computation | async-start | bytes 524288 | tf_op jit(solution)/shard_map/psum | solution.py:49
  27.1 16.6 %copy-start.2 = (bf16[2048]{0:T(1024)(128)(2,1)S(1)}, bf16[2048]{0:T(1024)(128)(2,1)}, u32[]{:S(2)}) copy-start(bf16[2048]{0:T(1024)(128)(2,1)} %param.16) | copy-start | bytes 12292
  27.1 86.6 %copy-start.1 = (bf16[64,2048]{1,0:T(8,128)(2,1)S(1)}, bf16[64,2048]{1,0:T(8,128)(2,1)}, u32[]{:S(2)}) copy-start(bf16[64,2048]{1,0:T(8,128)(2,1)} %param.10) | copy-start | bytes 786436
  43.6 142.1 %all-reduce.5.cloned.1.call-start = ((), (), s32[]{:S(2)}) async-start(), calls=%async_computation.1 | async-start | bytes 524288 | tf_op jit(solution)/shard_map/psum | solution.py:49
Sparse Core Ops, SparseCore 0:
  43.7 69.9 all-reduce.2
  120.9 64.6 all-reduce.4
where the time goes:
time: 195 us; the launch traced here: 194 us
  waiting for transfers between devices  135 us (69%)
  matrix products  37.7 us (19%)
  between operations  13.5 us (7%)
  other arithmetic  7.62 us (4%)
    psum x2, waiting for transfers between devices, added(): lax.psum(term.astype(jnp.bfloat16), 'tp').astype(jnp.float32)  135 us
    dot_general x2, matrix products, einsum(): return jnp.einsum(form, a.astype(jnp.float32), b.astype(jnp.float32))  27.9 us
  transfers between devices with their start and end apart: 2, of which 2 were waited for; matrix products, arithmetic and copies ran while one was open for 0% of the time, Pallas kernels for 0%

commit v1 on v0

v1 whole, which is shorter than its diff:
```python
import functools

import jax
import jax.numpy as jnp
import numpy as np
from jax import lax
from jax.experimental import pallas as pl
from jax.experimental.pallas import tpu as pltpu
from jax.sharding import PartitionSpec as P

HEAD = 64
THETA = 10000
EPS = 1e-6
SEQS = 4
SLOTS = 8
MLP_AT = 11
SUM_AT = 14

F32, BF16 = jnp.float32, jnp.bfloat16
MESH = pl.DeviceIdType.MESH


def dot(a, b):
    return jnp.dot(a, b, preferred_element_type=F32)


def dot_t(a, b):
    return lax.dot_general(a, b, (((1,), (1,)), ((), ())), preferred_element_type=F32)


def normed(wide, gain):
    scale = lax.rsqrt(jnp.mean(wide * wide, -1, keepdims=True) + EPS)
    return wide * scale * gain


def kernel(
    n, heads, axis,
    x_hbm, k_hbm, v_hbm, ga_hbm, wq_hbm, wo_hbm, gm_hbm, wg_hbm, wu_hbm, wd_hbm, rope_hbm,
    y_ref,
    xs, x_own, ga, gm, rope, wq, wo, wg, wu, wd,
    kbuf, vbuf, qbd, s_ref, terms, landed, h_all, b_ref, own2, terms2, landed2, y_all,
    k_sem, v_sem, w_sem, send1, recv1, send2, recv2, send3, recv3, send4, recv4,
):
    me = lax.axis_index(axis)
    width = heads * HEAD
    rows = SEQS * heads
    batch = x_hbm.shape[0] * x_hbm.shape[1]
    steps = batch // SEQS
    parts = steps // n
    cache = k_hbm.shape[-1]

    def peer(p):
        return lax.rem(me + p, n)

    def block_of(g):
        return lax.rem(me + 1 + lax.rem(g, n), n)

    def group_of(g):
        return block_of(g) * parts + g // n

    def k_copy(g):
        return pltpu.make_async_copy(k_hbm.at[group_of(g)], kbuf.at[lax.rem(g, SLOTS)], k_sem.at[lax.rem(g, SLOTS)])

    def v_copy(g):
        return pltpu.make_async_copy(v_hbm.at[group_of(g)], vbuf.at[lax.rem(g, SLOTS)], v_sem.at[lax.rem(g, SLOTS)])

    first = [
        pltpu.make_async_copy(x_hbm, xs, w_sem.at[0]),
        pltpu.make_async_copy(ga_hbm, ga, w_sem.at[1]),
        pltpu.make_async_copy(wq_hbm, wq, w_sem.at[2]),
        pltpu.make_async_copy(rope_hbm, rope, w_sem.at[3]),
    ]
    second = [pltpu.make_async_copy(wo_hbm, wo, w_sem.at[4]), pltpu.make_async_copy(x_hbm.at[me], x_own, w_sem.at[5])]
    third = [
        pltpu.make_async_copy(wg_hbm, wg, w_sem.at[6]),
        pltpu.make_async_copy(wu_hbm, wu, w_sem.at[7]),
        pltpu.make_async_copy(wd_hbm, wd, w_sem.at[8]),
        pltpu.make_async_copy(gm_hbm, gm, w_sem.at[9]),
    ]

    for c in first:
        c.start()
    k_copy(0).start()
    v_copy(0).start()
    for c in second:
        c.start()
    for g in range(1, SLOTS):
        k_copy(g).start()
        v_copy(g).start()
    k_tail = SLOTS

    barrier = pltpu.get_barrier_semaphore()
    for p in range(1, n):
        pl.semaphore_signal(barrier, inc=1, device_id={axis: peer(p)}, device_id_type=MESH)

    for c in first:
        c.wait()
    a = normed(xs[...].reshape(batch, -1).astype(F32), ga[...].astype(F32)).astype(BF16)
    q = dot(a, wq[...]).astype(BF16).astype(F32)
    lane = lax.broadcasted_iota(jnp.int32, q.shape, 1)
    half = HEAD // 2
    low = lax.rem(lane, HEAD) < half
    other = jnp.where(low, pltpu.roll(q, width - half, 1), pltpu.roll(q, half, 1))
    q = (q * rope[0:1, :] + other * rope[1:2, :]).astype(BF16)
    r = lax.broadcasted_iota(jnp.int32, (steps * rows, batch), 0)
    t = lax.broadcasted_iota(jnp.int32, (steps * rows, batch), 1)
    pick = jnp.where(t == (r // rows) * SEQS + lax.rem(r, SEQS), 1.0, 0.0).astype(BF16)
    r = lax.broadcasted_iota(jnp.int32, (steps * rows, width), 0)
    c = lax.broadcasted_iota(jnp.int32, (steps * rows, width), 1)
    spread = jnp.where(c // HEAD == lax.rem(r // SEQS, heads), dot(pick, q), 0.0).astype(BF16)
    qbd[...] = spread.reshape(steps, rows, width)

    row = lax.broadcasted_iota(jnp.int32, (rows, cache), 0)
    vrow = lax.broadcasted_iota(jnp.int32, (width, rows), 0)
    vcol = lax.broadcasted_iota(jnp.int32, (width, rows), 1)
    fold_r = lax.broadcasted_iota(jnp.int32, (8, rows), 0)
    fold_c = lax.broadcasted_iota(jnp.int32, (8, rows), 1)
    fold = jnp.where(lax.rem(fold_c, SEQS) == fold_r, 1.0, 0.0).astype(BF16)

    def scores(g):
        slot = lax.rem(g, SLOTS)
        qs = qbd[group_of(g)]
        s = dot(qs, kbuf[slot, 0])
        for i in range(1, SEQS):
            s = jnp.where(lax.rem(row, SEQS) == i, dot(qs, kbuf[slot, i]), s)
        return s

    def weights():
        s = s_ref[...]
        e = jnp.exp((s - jnp.max(s, -1, keepdims=True)) * HEAD**-0.5)
        return (e * (1.0 / jnp.sum(e, -1, keepdims=True))).astype(BF16)

    def attended(g, w):
        slot = lax.rem(g, SLOTS)
        acc = jnp.zeros((width, rows), F32)
        for i in range(SEQS):
            acc = jnp.where(vcol == (vrow // HEAD) * SEQS + i, dot_t(vbuf[slot, i], w), acc)
        return dot_t(fold, acc.astype(BF16)).astype(BF16)

    def term1(g, to):
        return pltpu.make_async_remote_copy(
            terms.at[g], landed.at[g], send1.at[g], recv1.at[g], device_id={axis: to}, device_id_type=MESH
        )

    def gather1(b, p):
        return pltpu.make_async_remote_copy(
            h_all.at[b, me], h_all.at[b, me], send2.at[b, p], recv2.at[b, p], device_id={axis: peer(p)}, device_id_type=MESH
        )

    def term2(b, p):
        return pltpu.make_async_remote_copy(
            terms2.at[b, peer(p)], landed2.at[b, p], send3.at[b, p], recv3.at[b, p], device_id={axis: peer(p)}, device_id_type=MESH
        )

    def gather2(b, p):
        return pltpu.make_async_remote_copy(
            y_all.at[b, me], y_all.at[b, me], send4.at[b, p], recv4.at[b, p], device_id={axis: peer(p)}, device_id_type=MESH
        )

    far_first = sorted(range(1, n), key=lambda p: -min(p, n - p))

    def finish_h(b, own):
        h = x_own[...].astype(F32)[b * SEQS : (b + 1) * SEQS] + own
        for k in range(n - 1):
            term1(b * n + k, me).wait_recv()
            h = h + landed[b * n + k].astype(F32)
        h_all[b, me] = h.astype(BF16)
        for p in far_first:
            gather1(b, p).start()

    def mlp(b):
        for p in far_first:
            pltpu.make_async_remote_copy(
                h_all.at[b, peer(n - p)], h_all.at[b, peer(n - p)], send2.at[b, p], recv2.at[b, p],
                device_id={axis: peer(p)}, device_id_type=MESH,
            ).wait_recv()
        gain = gm[...].astype(F32)
        for j in range(n):
            b_ref[j * SEQS : (j + 1) * SEQS, :] = normed(h_all[b, j].astype(F32), gain)
        states = b_ref[...].astype(BF16)
        gate, up = dot(states, wg[...]), dot(states, wu[...])
        hidden = (gate * (1.0 / (1.0 + jnp.exp(-gate))) * up).astype(BF16)
        part = dot(hidden, wd[...])
        for j in range(n):
            mine = part[j * SEQS : (j + 1) * SEQS]
            own2[j] = mine
            terms2[b, j] = mine.astype(BF16)
        for p in far_first:
            term2(b, p).start()

    def finish_y(b):
        y = h_all[b, me].astype(F32) + own2[me]
        for p in far_first:
            term2(b, p).wait_recv()
            y = y + landed2[b, p].astype(F32)
        y_all[b, me] = y.astype(BF16)
        for p in far_first:
            gather2(b, p).start()

    k_copy(0).wait()
    s_ref[...] = scores(0)
    k_copy(k_tail).start()
    for c in second:
        c.wait()
    pl.semaphore_wait(barrier, n - 1)

    def body(g, carry):
        @pl.when(g == 2)
        def _():
            for c in third:
                c.start()

        if parts > 1:

            @pl.when(g == MLP_AT)
            def _():
                for c in third:
                    c.wait()
                mlp(0)

            @pl.when(g == SUM_AT)
            def _():
                finish_y(0)

        k_copy(g + 1).wait()
        v_copy(g).wait()
        w = weights()
        s = scores(g + 1)
        part = dot(attended(g, w), wo[...])[:SEQS]
        s_ref[...] = s

        @pl.when(g + 1 + SLOTS < steps)
        def _():
            k_copy(g + 1 + SLOTS).start()

        @pl.when(g + SLOTS < steps)
        def _():
            v_copy(g + SLOTS).start()

        last = lax.rem(g, n) == n - 1

        @pl.when(jnp.logical_not(last))
        def _():
            terms[g] = part.astype(BF16)
            term1(g, block_of(g)).start()

        @pl.when(last)
        def _():
            finish_h(0, part)

        return carry

    lax.fori_loop(0, steps - 1, body, 0)
    g = steps - 1
    v_copy(g).wait()
    finish_h(parts - 1, dot(attended(g, weights()), wo[...])[:SEQS])
    mlp(parts - 1)
    finish_y(parts - 1)

    for b in range(parts):
        for p in far_first:
            pltpu.make_async_remote_copy(
                y_all.at[b, peer(n - p)], y_all.at[b, peer(n - p)], send4.at[b, p], recv4.at[b, p],
                device_id={axis: peer(p)}, device_id_type=MESH,
            ).wait_recv()
    for j in range(n):
        y_ref[j] = jnp.concatenate([y_all[b, j].astype(F32) for b in range(parts)], 0).astype(BF16)

    for b in range(parts):
        for k in range(n - 1):
            term1(b * n + k, me).wait_send()
        for p in far_first:
            gather1(b, p).wait_send()
            term2(b, p).wait_send()
            gather2(b, p).wait_send()


def solution(mesh):
    n = mesh.shape["tp"]

    def step(x, k_cache, v_cache, gain_a, wq, wo, gain_m, w_gate, w_up, w_down):
        batch, d = x.shape
        cache, heads = k_cache.shape[1:3]
        width, ff = heads * HEAD, w_gate.shape[1]
        steps = batch // SEQS
        parts = steps // n

        def turned_round(c):
            return c.transpose(0, 2, 3, 1).reshape(steps, SEQS, width, cache)

        half = HEAD // 2
        angle = (cache - 1) * THETA ** (-np.arange(half, dtype=np.float64) / half)
        cos, sin = np.cos(angle), np.sin(angle)
        rope = np.stack([np.tile(np.concatenate([cos, cos]), heads), np.tile(np.concatenate([-sin, sin]), heads)])
        rope = jnp.asarray(rope.astype(np.float32))

        dma = pltpu.SemaphoreType.DMA
        out = pl.pallas_call(
            functools.partial(kernel, n, heads, "tp"),
            out_shape=jax.ShapeDtypeStruct((n, batch // n, d), BF16),
            in_specs=[pl.BlockSpec(memory_space=pl.ANY)] * 11,
            out_specs=pl.BlockSpec(memory_space=pltpu.VMEM),
            scratch_shapes=[
                pltpu.VMEM((n, batch // n, d), BF16),
                pltpu.VMEM((batch // n, d), BF16),
                pltpu.VMEM((1, d), BF16),
                pltpu.VMEM((1, d), BF16),
                pltpu.VMEM((2, width), F32),
                pltpu.VMEM(wq.shape, BF16),
                pltpu.VMEM(wo.shape, BF16),
                pltpu.VMEM(w_gate.shape, BF16),
                pltpu.VMEM(w_up.shape, BF16),
                pltpu.VMEM(w_down.shape, BF16),
                pltpu.VMEM((SLOTS, SEQS, width, cache), BF16),
                pltpu.VMEM((SLOTS, SEQS, width, cache), BF16),
                pltpu.VMEM((steps, SEQS * heads, width), BF16),
                pltpu.VMEM((SEQS * heads, cache), F32),
                pltpu.VMEM((steps, SEQS, d), BF16),
                pltpu.VMEM((steps, SEQS, d), BF16),
                pltpu.VMEM((parts, n, SEQS, d), BF16),
                pltpu.VMEM((n * SEQS, d), F32),
                pltpu.VMEM((n, SEQS, d), F32),
                pltpu.VMEM((parts, n, SEQS, d), BF16),
                pltpu.VMEM((parts, n, SEQS, d), BF16),
                pltpu.VMEM((parts, n, SEQS, d), BF16),
                dma((SLOTS,)),
                dma((SLOTS,)),
                dma((10,)),
                dma((steps,)),
                dma((steps,)),
            ]
            + [dma((parts, n))] * 6,
            compiler_params=pltpu.CompilerParams(collective_id=0, has_side_effects=True, vmem_limit_bytes=67043328),
        )(
            x.reshape(n, batch // n, d), turned_round(k_cache), turned_round(v_cache), gain_a.reshape(1, d), wq, wo,
            gain_m.reshape(1, d), w_gate, w_up, w_down, rope,
        )
        return out.reshape(batch, d)

    states, cache, columns, rows_of = P("dp", None), P("dp", None, "tp", None), P(None, "tp"), P("tp", None)
    return jax.shard_map(
        step,
        mesh=mesh,
        in_specs=(states, cache, cache, P(None), columns, rows_of, P(None), columns, columns, rows_of),
        out_specs=states,
        check_vma=False,
    )
```

time: 195 us -> 68.6 us (0.35)
  waiting for transfers between devices: 135 us -> 0 us
  Pallas kernels: 0 us -> 63.3 us
  matrix products: 37.7 us -> 0 us
  between operations: 13.5 us -> 0.01 us
  other arithmetic: 7.62 us -> 0 us
  local copies, waits for them, and re-layouts: 0.37 us -> 4.24 us
    psum x2 -> x0, waiting for transfers between devices: 135 us -> none  [added(): lax.psum(term.astype(jnp.bfloat16), 'tp').astype(jnp.float32)]
    pallas_call x0 -> x1, Pallas kernels: none -> 63.3 us  [step(): pl.pallas_call(functools.partial(kernel, n, heads, 'tp'), out_shape=jax.S...]
    dot_general x6 -> x0, matrix products: 37.7 us -> none  [the longest x2 27.9 us: einsum(): return jnp.einsum(form, a.astype(jnp.float32), b.astype(jnp.float32))]
    div x1 -> x0, other arithmetic: 2.62 us -> none  [seen_by(): weights = jax.nn.softmax(scores, -1).astype(jnp.bfloat16)]
    convert_element_type x4 -> x0, other arithmetic: 2.59 us -> none  [the longest x1 1.71 us: added(): (t.astype(jnp.float32) + lax.psum(term.astype(jnp.bfloat16), 'tp').astype...]
    reshape x1 -> x2, local copies, waits for them, and re-layouts: 0.11 us -> 2.57 us  [the longest x1 1.29 us: step(): gain_a.reshape(1, d)]
    reduce_sum x2 -> x0, other arithmetic: 2.24 us -> none  [normed(): scale = lax.rsqrt(jnp.mean(wide * wide, -1, keepdims=True) + 1e-06)]
  transfers between devices with their start and end apart: 2 -> 0, of which waited for: 2 -> 0; matrix products, arithmetic and copies ran while one was open for 0% -> 0% of each run, Pallas kernels for 0% -> 0%
where the time goes in v1:
time: 68.6 us; the launch traced here: 67.6 us
  Pallas kernels  63.3 us (92%)
  local copies, waits for them, and re-layouts  4.24 us (6%)
    pallas_call x1, Pallas kernels, step(): pl.pallas_call(functools.partial(kernel, n, heads, 'tp'), out_shape=jax.S...  63.3 us
    unnamed x1, local copies, waits for them, and re-layouts  1.67 us

profile of v1, /device:TPU:28, one launch (start us, length us, event | category | flops | bytes accessed | tf_op | source)
XLA Modules:
  0.0 67.6 jit_solution(7229727248651182766)
XLA Ops:
  0.0 1.3 %reshape.21.ga_hbm = bf16[1,2048]{1,0:T(2,128)(2,1)} reshape(bf16[2048]{0:T(1024)(128)(2,1)} %param.14) | data formatting | bytes 8192 | tf_op jit(solution)/shard_map/reshape | solution.py:335
  1.3 1.3 %reshape.22.gm_hbm = bf16[1,2048]{1,0:T(2,128)(2,1)} reshape(bf16[2048]{0:T(1024)(128)(2,1)} %param.17) | data formatting | bytes 8192 | tf_op jit(solution)/shard_map/reshape | solution.py:336
  2.6 63.3 %shard_map.109 = bf16[8,8,2048]{2,1,0:T(8,128)(2,1)} custom-call(bf16[8,8,2048]{2,1,0:T(8,128)(2,1)} %bitcast.11, bf16[16,4,256,1024]{3,2,1,0:T(8,128)(2,1)} %bitcast.8, bf16[16,4,256,1024]{3,2,1,0:T(8,128)(2,1)} %bitcast.9, bf16[1,2048]{1,0:T(2,128)(2,1)} %reshape.21.ga_hbm, bf16[2048,256]{1,0:T(8,128)(2,1)} %wq_hbm.1, bf16[256,2048]{1,0:T(8,128)(2,1)} %wo_hbm.1, ...), custom_call_target="tpu_custom_call" | custom-call | tf_op jit(solution)/shard_map/pallas_call | solution.py:298
  65.9 1.7 %copy.13 = bf16[64,2048]{1,0:T(8,128)(2,1)} copy(bf16[64,2048]{1,0:T(8,128)(2,1)} %bitcast.10) | data formatting | bytes 524288

commit v2 on v1

v2 whole, which is shorter than its diff:
```python
import functools

import jax
import jax.numpy as jnp
import numpy as np
from jax import lax
from jax.experimental import pallas as pl
from jax.experimental.pallas import tpu as pltpu
from jax.sharding import PartitionSpec as P

HEAD = 64
THETA = 10000
EPS = 1e-6
SEQS = 4
SLOTS = 4
MLP_AT = 13
TILE = 256

F32, BF16 = jnp.float32, jnp.bfloat16
MESH = pl.DeviceIdType.MESH


def dot(a, b):
    return jnp.dot(a, b, preferred_element_type=F32)


def dot_t(a, b):
    return lax.dot_general(a, b, (((1,), (1,)), ((), ())), preferred_element_type=F32)


def normed(wide, gain):
    scale = lax.rsqrt(jnp.mean(wide * wide, -1, keepdims=True) + EPS)
    return wide * scale * gain


def kernel(
    n, heads, axis,
    x_hbm, k_hbm, v_hbm, ga_hbm, wq_hbm, wo_hbm, gm_hbm, wg_hbm, wu_hbm, wd_hbm, rope_hbm,
    y_ref,
    xs, ga, gm, rope, wq, wo, wg, wu, wd,
    kbuf, vbuf, qcat, p_ref, o_ref, terms, landed, h_own, h_in, b_ref, own2, terms2, landed2, y_all,
    k_sem, v_sem, w_sem, send1, recv1, send2, recv2, send3, recv3, send4, recv4,
):
    me = lax.axis_index(axis)
    width = heads * HEAD
    rows = SEQS * heads
    batch = x_hbm.shape[0] * x_hbm.shape[1]
    steps = batch // SEQS
    parts = steps // n
    cache = k_hbm.shape[-1]
    d = x_hbm.shape[-1]

    def peer(p):
        return lax.rem(me + p, n)

    def block_of(g):
        return lax.rem(me + 1 + lax.rem(g, n), n)

    def group_of(g):
        return block_of(g) * parts + g // n

    def k_copy(g):
        return pltpu.make_async_copy(k_hbm.at[group_of(g)], kbuf.at[lax.rem(g, SLOTS)], k_sem.at[lax.rem(g, SLOTS)])

    def v_copy(g):
        return pltpu.make_async_copy(v_hbm.at[group_of(g)], vbuf.at[lax.rem(g, SLOTS)], v_sem.at[lax.rem(g, SLOTS)])

    first = [
        pltpu.make_async_copy(x_hbm, xs, w_sem.at[0]),
        pltpu.make_async_copy(ga_hbm, ga, w_sem.at[1]),
        pltpu.make_async_copy(wq_hbm, wq, w_sem.at[2]),
        pltpu.make_async_copy(rope_hbm, rope, w_sem.at[3]),
    ]
    wo_copy = pltpu.make_async_copy(wo_hbm, wo, w_sem.at[4])
    third = [
        pltpu.make_async_copy(wg_hbm, wg, w_sem.at[5]),
        pltpu.make_async_copy(wu_hbm, wu, w_sem.at[6]),
        pltpu.make_async_copy(wd_hbm, wd, w_sem.at[7]),
        pltpu.make_async_copy(gm_hbm, gm, w_sem.at[8]),
    ]

    for c in first:
        c.start()
    k_copy(0).start()
    wo_copy.start()
    v_copy(0).start()
    k_copy(1).start()

    barrier = pltpu.get_barrier_semaphore()
    for p in range(1, n):
        pl.semaphore_signal(barrier, inc=1, device_id={axis: peer(p)}, device_id_type=MESH)

    with jax.named_scope("first_wait"):
        for c in first:
            c.wait()
    v_copy(1).start()
    for g in range(2, SLOTS):
        k_copy(g).start()
        v_copy(g).start()

    a = normed(xs[...].reshape(batch, -1).astype(F32), ga[...].astype(F32)[None]).astype(BF16)
    q = dot(a, wq[...]).astype(BF16).astype(F32)
    lane = lax.broadcasted_iota(jnp.int32, q.shape, 1)
    half = HEAD // 2
    low = lax.rem(lane, HEAD) < half
    other = jnp.where(low, pltpu.roll(q, width - half, 1), pltpu.roll(q, half, 1))
    q = (q * rope[0:1, :] + other * rope[1:2, :]).astype(BF16)
    r = lax.broadcasted_iota(jnp.int32, (steps * rows, batch), 0)
    t = lax.broadcasted_iota(jnp.int32, (steps * rows, batch), 1)
    pick = jnp.where(t == (r // rows) * SEQS + lax.rem(r, SEQS), 1.0, 0.0).astype(BF16)
    r = lax.broadcasted_iota(jnp.int32, (steps * rows, width), 0)
    c = lax.broadcasted_iota(jnp.int32, (steps * rows, width), 1)
    spread = jnp.where(c // HEAD == lax.rem(r // SEQS, heads), dot(pick, q), 0.0)
    for i in range(SEQS):
        qcat[:, :, i * width : (i + 1) * width] = (
            jnp.where(lax.rem(r, SEQS) == i, spread, 0.0).astype(BF16).reshape(steps, rows, width)
        )

    row = lax.broadcasted_iota(jnp.int32, (rows, cache), 0)
    vrow = lax.broadcasted_iota(jnp.int32, (width, rows), 0)
    vcol = lax.broadcasted_iota(jnp.int32, (width, rows), 1)
    fold_r = lax.broadcasted_iota(jnp.int32, (8, rows), 0)
    fold_c = lax.broadcasted_iota(jnp.int32, (8, rows), 1)
    fold = jnp.where(lax.rem(fold_c, SEQS) == fold_r, 1.0, 0.0).astype(BF16)
    tiles = cache // TILE

    def score_pieces(g):
        slot, group = lax.rem(g, SLOTS), group_of(g)
        out = [None] * tiles

        def piece(t, i):
            x = dot(qcat[group, :, i * width : (i + 1) * width], kbuf[slot, i, :, t * TILE : (t + 1) * TILE])
            out[t] = x if out[t] is None else out[t] + x

        order = [(t, i) for u in range(0, tiles, 2) for i in range(SEQS) for t in range(u, min(u + 2, tiles))]
        return [functools.partial(piece, t, i) for t, i in order], out

    def value_pieces(g):
        slot = lax.rem(g, SLOTS)
        out = [None, None]

        def piece(c, i, t):
            x = dot_t(vbuf[slot, i, :, t * TILE : (t + 1) * TILE], p_ref[i, :, t * TILE : (t + 1) * TILE])
            out[c] = x if out[c] is None else out[c] + x

        order = [(c, c * SEQS // 2 + i, t) for i in range(SEQS // 2) for t in range(tiles) for c in range(2)]
        return [functools.partial(piece, *o) for o in order], out

    def store_weights(s):
        e = jnp.exp((s - jnp.max(s, -1, keepdims=True)) * HEAD**-0.5)
        w = e * (1.0 / jnp.sum(e, -1, keepdims=True))
        for i in range(SEQS):
            p_ref[i] = jnp.where(lax.rem(row, SEQS) == i, w, 0.0).astype(BF16)

    def folded(sums):
        acc = jnp.where(vcol // SEQS == vrow // HEAD, sums[0] + sums[1], 0.0)
        return dot_t(fold, acc.astype(BF16)).astype(BF16)

    def term1(b, k, to):
        return pltpu.make_async_remote_copy(
            terms.at[b, k], landed.at[b, k], send1.at[b], recv1.at[b], device_id={axis: to}, device_id_type=MESH
        )

    def gather1(b, p):
        return pltpu.make_async_remote_copy(
            h_own.at[b], h_in.at[b, p - 1], send2.at[b], recv2.at[b], device_id={axis: peer(p)}, device_id_type=MESH
        )

    def term2(b, p):
        return pltpu.make_async_remote_copy(
            terms2.at[b, p - 1], landed2.at[b, p - 1], send3.at[b], recv3.at[b], device_id={axis: peer(n - p)}, device_id_type=MESH
        )

    def gather2(b, p):
        return pltpu.make_async_remote_copy(
            y_all.at[b, me], y_all.at[b, me], send4.at[b], recv4.at[b], device_id={axis: peer(p)}, device_id_type=MESH
        )

    def all_of(ref, b, send, recv):
        some = ref.at[b, pl.ds(0, n - 1)]
        return pltpu.make_async_remote_copy(some, some, send.at[b], recv.at[b], device_id={axis: me}, device_id_type=MESH)

    far_first = sorted(range(1, n), key=lambda p: -min(p, n - p))

    def finish_h(b, own):
        h = xs[me].astype(F32)[b * SEQS : (b + 1) * SEQS] + own
        with jax.named_scope(f"term1_wait#b={b}"):
            all_of(landed, b, send1, recv1).wait_recv()
        for k in range(n - 1):
            h = h + landed[b, k].astype(F32)
        h_own[b] = h.astype(BF16)
        for p in far_first:
            gather1(b, p).start()

    def mlp(b):
        with jax.named_scope(f"gather1_wait#b={b}"):
            all_of(h_in, b, send2, recv2).wait_recv()
        gain = gm[...].astype(F32)[None]
        for j in range(n):
            b_ref[j * SEQS : (j + 1) * SEQS, :] = normed((h_in[b, j - 1] if j else h_own[b]).astype(F32), gain)
        states = b_ref[...].astype(BF16)
        gate, up = dot(states, wg[...]), dot(states, wu[...])
        hidden = (gate * (1.0 / (1.0 + jnp.exp(-gate))) * up).astype(BF16)
        part = dot(hidden, wd[...])
        own2[b] = part[:SEQS]
        for j in range(1, n):
            terms2[b, j - 1] = part[j * SEQS : (j + 1) * SEQS].astype(BF16)
        for p in far_first:
            term2(b, p).start()

    def finish_y(b):
        y = h_own[b].astype(F32) + own2[b]
        with jax.named_scope(f"term2_wait#b={b}"):
            all_of(landed2, b, send3, recv3).wait_recv()
        for p in range(1, n):
            y = y + landed2[b, p - 1].astype(F32)
        y_all[b, me] = y.astype(BF16)
        for p in far_first:
            gather2(b, p).start()

    with jax.named_scope("k0_wait"):
        k_copy(0).wait()
    todo, s = score_pieces(0)
    for piece in todo:
        piece()
    store_weights(jnp.concatenate(s, 1))
    o_ref[...] = jnp.zeros_like(o_ref)
    k_copy(SLOTS).start()
    with jax.named_scope("wo_wait"):
        wo_copy.wait()
    with jax.named_scope("barrier_wait"):
        pl.semaphore_wait(barrier, n - 1)

    def send_term(g, part):
        terms[g // n, lax.rem(g, n)] = part.astype(BF16)
        term1(g // n, lax.rem(g, n), block_of(g)).start()

    def body(g, carry):
        @pl.when(g == 2)
        def _():
            for c in third:
                c.start()

        if parts > 1:

            @pl.when(g == MLP_AT)
            def _():
                with jax.named_scope("third_wait"):
                    for c in third:
                        c.wait()
                mlp(0)

        with jax.named_scope("kv_wait"):
            k_copy(g + 1).wait()
            v_copy(g).wait()
        ks, s = score_pieces(g + 1)
        vs, sums = value_pieces(g)
        before = o_ref[...]
        part = []
        for j in range(len(vs)):
            for piece in ks[2 * j : 2 * j + 2]:
                piece()
            vs[j]()
            if j % 2:
                part.append(dot(before, wo[:, j // 2 * TILE : (j // 2 + 1) * TILE]))
        o_ref[...] = folded(sums)
        store_weights(jnp.concatenate(s, 1))
        part = jnp.concatenate(part, 1)[:SEQS]

        @pl.when(g + 1 + SLOTS < steps)
        def _():
            k_copy(g + 1 + SLOTS).start()

        @pl.when(g + SLOTS < steps)
        def _():
            v_copy(g + SLOTS).start()

        own_before = lax.rem(g, n) == 0

        @pl.when(jnp.logical_not(own_before))
        def _():
            send_term(g - 1, part)

        @pl.when(jnp.logical_and(own_before, g > 0))
        def _():
            finish_h(0, part)

        return carry

    lax.fori_loop(0, steps - 1, body, 0)
    g = steps - 1
    send_term(g - 1, dot(o_ref[...], wo[...])[:SEQS])
    v_copy(g).wait()
    vs, sums = value_pieces(g)
    for piece in vs:
        piece()
    finish_h(parts - 1, dot(folded(sums), wo[...])[:SEQS])
    for b in range(parts - 1):
        finish_y(b)
    mlp(parts - 1)
    finish_y(parts - 1)

    with jax.named_scope("gather2_wait"):
        for b in range(parts):
            all_of(y_all, b, send4, recv4).wait_recv()
    for j in range(n):
        y_ref[j] = jnp.concatenate([y_all[b, j].astype(F32) for b in range(parts)], 0).astype(BF16)

    with jax.named_scope("send_wait"):
        for b in range(parts):
            all_of(terms, b, send1, recv1).wait_send()
            all_of(h_in, b, send2, recv2).wait_send()
            all_of(terms2, b, send3, recv3).wait_send()
            all_of(y_all, b, send4, recv4).wait_send()


def solution(mesh):
    n = mesh.shape["tp"]

    def step(x, k_cache, v_cache, gain_a, wq, wo, gain_m, w_gate, w_up, w_down):
        batch, d = x.shape
        cache, heads = k_cache.shape[1:3]
        width, ff = heads * HEAD, w_gate.shape[1]
        steps = batch // SEQS
        parts = steps // n
        rows = SEQS * heads

        def turned_round(c):
            return c.transpose(0, 2, 3, 1).reshape(steps, SEQS, width, cache)

        half = HEAD // 2
        angle = (cache - 1) * THETA ** (-np.arange(half, dtype=np.float64) / half)
        cos, sin = np.cos(angle), np.sin(angle)
        rope = np.stack([np.tile(np.concatenate([cos, cos]), heads), np.tile(np.concatenate([-sin, sin]), heads)])
        rope = jnp.asarray(rope.astype(np.float32))

        dma = pltpu.SemaphoreType.DMA
        out = pl.pallas_call(
            functools.partial(kernel, n, heads, "tp"),
            out_shape=jax.ShapeDtypeStruct((n, batch // n, d), BF16),
            in_specs=[pl.BlockSpec(memory_space=pl.ANY)] * 11,
            out_specs=pl.BlockSpec(memory_space=pltpu.VMEM),
            scratch_shapes=[
                pltpu.VMEM((n, batch // n, d), BF16),
                pltpu.VMEM((d,), BF16),
                pltpu.VMEM((d,), BF16),
                pltpu.VMEM((2, width), F32),
                pltpu.VMEM(wq.shape, BF16),
                pltpu.VMEM(wo.shape, BF16),
                pltpu.VMEM(w_gate.shape, BF16),
                pltpu.VMEM(w_up.shape, BF16),
                pltpu.VMEM(w_down.shape, BF16),
                pltpu.VMEM((SLOTS, SEQS, width, cache), BF16),
                pltpu.VMEM((SLOTS, SEQS, width, cache), BF16),
                pltpu.VMEM((steps, rows, SEQS * width), BF16),
                pltpu.VMEM((SEQS, rows, cache), BF16),
                pltpu.VMEM((8, width), BF16),
                pltpu.VMEM((parts, n - 1, SEQS, d), BF16),
                pltpu.VMEM((parts, n - 1, SEQS, d), BF16),
                pltpu.VMEM((parts, SEQS, d), BF16),
                pltpu.VMEM((parts, n - 1, SEQS, d), BF16),
                pltpu.VMEM((n * SEQS, d), F32),
                pltpu.VMEM((parts, SEQS, d), F32),
                pltpu.VMEM((parts, n - 1, SEQS, d), BF16),
                pltpu.VMEM((parts, n - 1, SEQS, d), BF16),
                pltpu.VMEM((parts, n, SEQS, d), BF16),
                dma((SLOTS,)),
                dma((SLOTS,)),
                dma((9,)),
            ]
            + [dma((parts,))] * 8,
            compiler_params=pltpu.CompilerParams(collective_id=0, has_side_effects=True, vmem_limit_bytes=67043328),
        )(
            x.reshape(n, batch // n, d), turned_round(k_cache), turned_round(v_cache), gain_a, wq, wo,
            gain_m, w_gate, w_up, w_down, rope,
        )
        return out.reshape(batch, d)

    states, cache, columns, rows_of = P("dp", None), P("dp", None, "tp", None), P(None, "tp"), P("tp", None)
    return jax.shard_map(
        step,
        mesh=mesh,
        in_specs=(states, cache, cache, P(None), columns, rows_of, P(None), columns, columns, rows_of),
        out_specs=states,
        check_vma=False,
    )
```

time: 68.6 us -> 58.3 us (0.85)
  Pallas kernels: 63.3 us -> 55.8 us
  local copies, waits for them, and re-layouts: 4.24 us -> 1.67 us
    pallas_call x1, Pallas kernels: 63.3 us -> 55.8 us  [step(): pl.pallas_call(functools.partial(kernel, n, heads, 'tp'), out_shape=jax.S...]
    reshape x2 -> x0, local copies, waits for them, and re-layouts: 2.57 us -> none  [the longest x1 1.29 us: step(): gain_a.reshape(1, d)]
where the time goes in v2:
time: 58.3 us; the launch traced here: 57.5 us
  Pallas kernels  55.8 us (96%)
  local copies, waits for them, and re-layouts  1.67 us (3%)
    pallas_call x1, Pallas kernels, step(): pl.pallas_call(functools.partial(kernel, n, heads, 'tp'), out_shape=jax.S...  55.8 us
    unnamed x1, local copies, waits for them, and re-layouts  1.67 us

profile of v2, /device:TPU:28, one launch (start us, length us, event | category | flops | bytes accessed | tf_op | source)
XLA Modules:
  0.0 57.5 jit_solution(3603216191942305209)
XLA Ops:
  0.0 55.8 %shard_map.109 = bf16[8,8,2048]{2,1,0:T(8,128)(2,1)} custom-call(bf16[8,8,2048]{2,1,0:T(8,128)(2,1)} %bitcast.11, bf16[16,4,256,1024]{3,2,1,0:T(8,128)(2,1)} %bitcast.8, bf16[16,4,256,1024]{3,2,1,0:T(8,128)(2,1)} %bitcast.9, bf16[2048]{0:T(1024)(128)(2,1)} %ga_hbm.1, bf16[2048,256]{1,0:T(8,128)(2,1)} %wq_hbm.1, bf16[256,2048]{1,0:T(8,128)(2,1)} %wo_hbm.1, ...), custom_call_target="tpu_custom_call" | custom-call | tf_op jit(solution)/shard_map/pallas_call | solution.py:338
  55.8 1.7 %copy.13 = bf16[64,2048]{1,0:T(8,128)(2,1)} copy(bf16[64,2048]{1,0:T(8,128)(2,1)} %bitcast.10) | data formatting | bytes 524288

commit v3 on v2

--- a/solution.py
+++ b/solution.py
@@ -13,8 +13,8 @@
 EPS = 1e-6
 SEQS = 4
 SLOTS = 4
-MLP_AT = 13
 TILE = 256
+VMEM_LIMIT = 44 * 2**20
 
 F32, BF16 = jnp.float32, jnp.bfloat16
 MESH = pl.DeviceIdType.MESH
@@ -193,7 +193,7 @@
             gather1(b, p).start()
 
     def mlp(b):
-        with jax.named_scope(f"gather1_wait#b={b}"):
+        with jax.named_scope("gather1_wait"):
             all_of(h_in, b, send2, recv2).wait_recv()
         gain = gm[...].astype(F32)[None]
         for j in range(n):
@@ -210,7 +210,7 @@
 
     def finish_y(b):
         y = h_own[b].astype(F32) + own2[b]
-        with jax.named_scope(f"term2_wait#b={b}"):
+        with jax.named_scope("term2_wait"):
             all_of(landed2, b, send3, recv3).wait_recv()
         for p in range(1, n):
             y = y + landed2[b, p - 1].astype(F32)
@@ -236,19 +236,10 @@
         term1(g // n, lax.rem(g, n), block_of(g)).start()
 
     def body(g, carry):
-        @pl.when(g == 2)
+        @pl.when(g == steps - SLOTS)
         def _():
             for c in third:
                 c.start()
-
-        if parts > 1:
-
-            @pl.when(g == MLP_AT)
-            def _():
-                with jax.named_scope("third_wait"):
-                    for c in third:
-                        c.wait()
-                mlp(0)
 
         with jax.named_scope("kv_wait"):
             k_copy(g + 1).wait()
@@ -289,16 +280,38 @@
 
     lax.fori_loop(0, steps - 1, body, 0)
     g = steps - 1
-    send_term(g - 1, dot(o_ref[...], wo[...])[:SEQS])
-    v_copy(g).wait()
-    vs, sums = value_pieces(g)
-    for piece in vs:
-        piece()
-    finish_h(parts - 1, dot(folded(sums), wo[...])[:SEQS])
-    for b in range(parts - 1):
+
+    @pl.when(me >= 0)
+    def _():
+        send_term(g - 1, dot(o_ref[...], wo[...])[:SEQS])
+        with jax.named_scope("last_v_wait"):
+            v_copy(g).wait()
+
+    @pl.when(me < n)
+    def _():
+        vs, sums = value_pieces(g)
+        for piece in vs:
+            piece()
+        o_ref[...] = folded(sums)
+
+    @pl.when(me > -1)
+    def _():
+        finish_h(parts - 1, dot(o_ref[...], wo[...])[:SEQS])
+
+    with jax.named_scope("third_wait"):
+        for c in third:
+            c.wait()
+
+    def each_mlp(b, carry):
+        mlp(b)
+        return carry
+
+    def each_y(b, carry):
         finish_y(b)
-    mlp(parts - 1)
-    finish_y(parts - 1)
+        return carry
+
+    lax.fori_loop(0, parts, each_mlp, 0)
+    lax.fori_loop(0, parts, each_y, 0)
 
     with jax.named_scope("gather2_wait"):
         for b in range(parts):
@@ -369,10 +382,15 @@
                 dma((9,)),
             ]
             + [dma((parts,))] * 8,
-            compiler_params=pltpu.CompilerParams(collective_id=0, has_side_effects=True, vmem_limit_bytes=67043328),
+            compiler_params=pltpu.CompilerParams(collective_id=0, has_side_effects=True, vmem_limit_bytes=VMEM_LIMIT),
         )(
-            x.reshape(n, batch // n, d), turned_round(k_cache), turned_round(v_cache), gain_a, wq, wo,
-            gain_m, w_gate, w_up, w_down, rope,
+            *(
+                pltpu.with_memory_space_constraint(t, pltpu.HBM)
+                for t in (
+                    x.reshape(n, batch // n, d), turned_round(k_cache), turned_round(v_cache), gain_a, wq, wo, gain_m,
+                    w_gate, w_up, w_down, rope,
+                )
+            )
         )
         return out.reshape(batch, d)
 

time: 58.3 us -> 52.1 us (0.89); the launches traced: 57.5 us -> 52 us
  Pallas kernels: 55.8 us -> 51.2 us
  local copies, waits for them, and re-layouts: 1.67 us -> 0.71 us
    pallas_call x1, Pallas kernels: 55.8 us -> 51.2 us  [step(): pl.pallas_call(functools.partial(kernel, n, heads, 'tp'), out_shape=jax.S...]
    unnamed x1, local copies, waits for them, and re-layouts: 1.67 us -> 0.71 us
where the time goes in v3:
time: 52.1 us; the launch traced here: 52 us
  Pallas kernels  51.2 us (98%)
  local copies, waits for them, and re-layouts  0.71 us (1%)
    pallas_call x1, Pallas kernels, step(): pl.pallas_call(functools.partial(kernel, n, heads, 'tp'), out_shape=jax.S...  51.2 us

profile of v3, /device:TPU:28, one launch (start us, length us, event | category | flops | bytes accessed | tf_op | source)
XLA Modules:
  0.0 52.0 jit_solution(6220591655426088761)
XLA Ops:
  0.0 51.2 %shard_map.109 = bf16[8,8,2048]{2,1,0:T(8,128)(2,1)S(1)} custom-call(bf16[8,8,2048]{2,1,0:T(8,128)(2,1)} %bitcast.11, bf16[16,4,256,1024]{3,2,1,0:T(8,128)(2,1)} %bitcast.9, bf16[16,4,256,1024]{3,2,1,0:T(8,128)(2,1)} %bitcast.10, bf16[2048]{0:T(1024)(128)(2,1)} %ga_hbm.1, bf16[2048,256]{1,0:T(8,128)(2,1)} %wq_hbm.1, bf16[256,2048]{1,0:T(8,128)(2,1)} %wo_hbm.1, ...), custom_call_target="tpu_custom_call" | custom-call | tf_op jit(solution)/shard_map/pallas_call | solution.py:351
  51.2 0.7 %copy.13 = bf16[64,2048]{1,0:T(8,128)(2,1)} copy(bf16[64,2048]{1,0:T(8,128)(2,1)S(1)} %bitcast.8) | data formatting | bytes 524288

commit v4 on v3

--- a/solution.py
+++ b/solution.py
@@ -14,6 +14,7 @@
 SEQS = 4
 SLOTS = 4
 TILE = 256
+MLP_AT = 13
 VMEM_LIMIT = 44 * 2**20
 
 F32, BF16 = jnp.float32, jnp.bfloat16
@@ -38,7 +39,7 @@
     x_hbm, k_hbm, v_hbm, ga_hbm, wq_hbm, wo_hbm, gm_hbm, wg_hbm, wu_hbm, wd_hbm, rope_hbm,
     y_ref,
     xs, ga, gm, rope, wq, wo, wg, wu, wd,
-    kbuf, vbuf, qcat, p_ref, o_ref, terms, landed, h_own, h_in, b_ref, own2, terms2, landed2, y_all,
+    kbuf, vbuf, qcat, p_ref, o_ref, terms, landed, h_own, b_own, b_in, b_ref, own2, terms2, landed2, y_all,
     k_sem, v_sem, w_sem, send1, recv1, send2, recv2, send3, recv3, send4, recv4,
 ):
     me = lax.axis_index(axis)
@@ -70,13 +71,13 @@
         pltpu.make_async_copy(ga_hbm, ga, w_sem.at[1]),
         pltpu.make_async_copy(wq_hbm, wq, w_sem.at[2]),
         pltpu.make_async_copy(rope_hbm, rope, w_sem.at[3]),
+        pltpu.make_async_copy(gm_hbm, gm, w_sem.at[8]),
     ]
     wo_copy = pltpu.make_async_copy(wo_hbm, wo, w_sem.at[4])
     third = [
         pltpu.make_async_copy(wg_hbm, wg, w_sem.at[5]),
         pltpu.make_async_copy(wu_hbm, wu, w_sem.at[6]),
         pltpu.make_async_copy(wd_hbm, wd, w_sem.at[7]),
-        pltpu.make_async_copy(gm_hbm, gm, w_sem.at[8]),
     ]
 
     for c in first:
@@ -163,7 +164,7 @@
 
     def gather1(b, p):
         return pltpu.make_async_remote_copy(
-            h_own.at[b], h_in.at[b, p - 1], send2.at[b], recv2.at[b], device_id={axis: peer(p)}, device_id_type=MESH
+            b_own.at[b], b_in.at[b, p - 1], send2.at[b], recv2.at[b], device_id={axis: peer(p)}, device_id_type=MESH
         )
 
     def term2(b, p):
@@ -188,16 +189,19 @@
             all_of(landed, b, send1, recv1).wait_recv()
         for k in range(n - 1):
             h = h + landed[b, k].astype(F32)
-        h_own[b] = h.astype(BF16)
+        h = h.astype(BF16)
+        h_own[b] = h
+        b_own[b] = normed(h.astype(F32), gm[...].astype(F32)[None]).astype(BF16)
         for p in far_first:
             gather1(b, p).start()
 
+    def wait_states(b):
+        with jax.named_scope("gather1_wait"):
+            all_of(b_in, b, send2, recv2).wait_recv()
+
     def mlp(b):
-        with jax.named_scope("gather1_wait"):
-            all_of(h_in, b, send2, recv2).wait_recv()
-        gain = gm[...].astype(F32)[None]
         for j in range(n):
-            b_ref[j * SEQS : (j + 1) * SEQS, :] = normed((h_in[b, j - 1] if j else h_own[b]).astype(F32), gain)
+            b_ref[j * SEQS : (j + 1) * SEQS, :] = (b_in[b, j - 1] if j else b_own[b]).astype(F32)
         states = b_ref[...].astype(BF16)
         gate, up = dot(states, wg[...]), dot(states, wu[...])
         hidden = (gate * (1.0 / (1.0 + jnp.exp(-gate))) * up).astype(BF16)
@@ -236,10 +240,21 @@
         term1(g // n, lax.rem(g, n), block_of(g)).start()
 
     def body(g, carry):
-        @pl.when(g == steps - SLOTS)
-        def _():
-            for c in third:
+        for at, c in zip((4, 6, 8), third):
+
+            @pl.when(g == at)
+            def _():
                 c.start()
+
+        if parts > 1:
+
+            @pl.when(g == MLP_AT)
+            def _():
+                with jax.named_scope("third_wait"):
+                    for c in third:
+                        c.wait()
+                wait_states(0)
+                mlp(0)
 
         with jax.named_scope("kv_wait"):
             k_copy(g + 1).wait()
@@ -298,20 +313,18 @@
     def _():
         finish_h(parts - 1, dot(o_ref[...], wo[...])[:SEQS])
 
-    with jax.named_scope("third_wait"):
+    if parts == 1:
         for c in third:
             c.wait()
-
-    def each_mlp(b, carry):
-        mlp(b)
-        return carry
-
-    def each_y(b, carry):
+    wait_states(parts - 1)
+    for b in range(parts - 1):
         finish_y(b)
-        return carry
-
-    lax.fori_loop(0, parts, each_mlp, 0)
-    lax.fori_loop(0, parts, each_y, 0)
+
+    @pl.when(me + 1 > 0)
+    def _():
+        mlp(parts - 1)
+
+    finish_y(parts - 1)
 
     with jax.named_scope("gather2_wait"):
         for b in range(parts):
@@ -322,7 +335,7 @@
     with jax.named_scope("send_wait"):
         for b in range(parts):
             all_of(terms, b, send1, recv1).wait_send()
-            all_of(h_in, b, send2, recv2).wait_send()
+            all_of(b_in, b, send2, recv2).wait_send()
             all_of(terms2, b, send3, recv3).wait_send()
             all_of(y_all, b, send4, recv4).wait_send()
 
@@ -371,6 +384,7 @@
                 pltpu.VMEM((parts, n - 1, SEQS, d), BF16),
                 pltpu.VMEM((parts, n - 1, SEQS, d), BF16),
                 pltpu.VMEM((parts, SEQS, d), BF16),
+                pltpu.VMEM((parts, SEQS, d), BF16),
                 pltpu.VMEM((parts, n - 1, SEQS, d), BF16),
                 pltpu.VMEM((n * SEQS, d), F32),
                 pltpu.VMEM((parts, SEQS, d), F32),

time: 52.1 us -> 54.2 us (1.040)
  Pallas kernels: 51.2 us -> 53.4 us
    pallas_call x1, Pallas kernels: 51.2 us -> 53.4 us  [step(): pl.pallas_call(functools.partial(kernel, n, heads, 'tp'), out_shape=jax.S...]
where the time goes in v4:
time: 54.2 us; the launch traced here: 54.1 us
  Pallas kernels  53.4 us (99%)
  local copies, waits for them, and re-layouts  0.71 us (1%)
    pallas_call x1, Pallas kernels, step(): pl.pallas_call(functools.partial(kernel, n, heads, 'tp'), out_shape=jax.S...  53.4 us

profile of v4, /device:TPU:28, one launch (start us, length us, event | category | flops | bytes accessed | tf_op | source)
XLA Modules:
  0.0 54.1 jit_solution(1040673801196128265)
XLA Ops:
  0.0 53.4 %shard_map.109 = bf16[8,8,2048]{2,1,0:T(8,128)(2,1)S(1)} custom-call(bf16[8,8,2048]{2,1,0:T(8,128)(2,1)} %bitcast.11, bf16[16,4,256,1024]{3,2,1,0:T(8,128)(2,1)} %bitcast.9, bf16[16,4,256,1024]{3,2,1,0:T(8,128)(2,1)} %bitcast.10, bf16[2048]{0:T(1024)(128)(2,1)} %ga_hbm.1, bf16[2048,256]{1,0:T(8,128)(2,1)} %wq_hbm.1, bf16[256,2048]{1,0:T(8,128)(2,1)} %wo_hbm.1, ...), custom_call_target="tpu_custom_call" | custom-call | tf_op jit(solution)/shard_map/pallas_call | solution.py:364
  53.4 0.7 %copy.13 = bf16[64,2048]{1,0:T(8,128)(2,1)} copy(bf16[64,2048]{1,0:T(8,128)(2,1)S(1)} %bitcast.8) | data formatting | bytes 524288

commit v5 on v3

--- a/solution.py
+++ b/solution.py
@@ -38,7 +38,7 @@
     x_hbm, k_hbm, v_hbm, ga_hbm, wq_hbm, wo_hbm, gm_hbm, wg_hbm, wu_hbm, wd_hbm, rope_hbm,
     y_ref,
     xs, ga, gm, rope, wq, wo, wg, wu, wd,
-    kbuf, vbuf, qcat, p_ref, o_ref, terms, landed, h_own, h_in, b_ref, own2, terms2, landed2, y_all,
+    kbuf, vbuf, qcat, p_ref, o_ref, terms, landed, h_own, b_own, b_in, b_ref, own2, terms2, landed2, y_all,
     k_sem, v_sem, w_sem, send1, recv1, send2, recv2, send3, recv3, send4, recv4,
 ):
     me = lax.axis_index(axis)
@@ -70,13 +70,13 @@
         pltpu.make_async_copy(ga_hbm, ga, w_sem.at[1]),
         pltpu.make_async_copy(wq_hbm, wq, w_sem.at[2]),
         pltpu.make_async_copy(rope_hbm, rope, w_sem.at[3]),
+        pltpu.make_async_copy(gm_hbm, gm, w_sem.at[8]),
     ]
     wo_copy = pltpu.make_async_copy(wo_hbm, wo, w_sem.at[4])
     third = [
         pltpu.make_async_copy(wg_hbm, wg, w_sem.at[5]),
         pltpu.make_async_copy(wu_hbm, wu, w_sem.at[6]),
         pltpu.make_async_copy(wd_hbm, wd, w_sem.at[7]),
-        pltpu.make_async_copy(gm_hbm, gm, w_sem.at[8]),
     ]
 
     for c in first:
@@ -119,32 +119,23 @@
     row = lax.broadcasted_iota(jnp.int32, (rows, cache), 0)
     vrow = lax.broadcasted_iota(jnp.int32, (width, rows), 0)
     vcol = lax.broadcasted_iota(jnp.int32, (width, rows), 1)
-    fold_r = lax.broadcasted_iota(jnp.int32, (8, rows), 0)
-    fold_c = lax.broadcasted_iota(jnp.int32, (8, rows), 1)
-    fold = jnp.where(lax.rem(fold_c, SEQS) == fold_r, 1.0, 0.0).astype(BF16)
-    tiles = cache // TILE
-
-    def score_pieces(g):
+    fold_r = lax.broadcasted_iota(jnp.int32, (2 * SEQS, rows), 0)
+    fold_c = lax.broadcasted_iota(jnp.int32, (2 * SEQS, rows), 1)
+    res_r = lax.broadcasted_iota(jnp.int32, (2 * SEQS, width), 0)
+
+    def scores(g):
         slot, group = lax.rem(g, SLOTS), group_of(g)
-        out = [None] * tiles
-
-        def piece(t, i):
-            x = dot(qcat[group, :, i * width : (i + 1) * width], kbuf[slot, i, :, t * TILE : (t + 1) * TILE])
-            out[t] = x if out[t] is None else out[t] + x
-
-        order = [(t, i) for u in range(0, tiles, 2) for i in range(SEQS) for t in range(u, min(u + 2, tiles))]
-        return [functools.partial(piece, t, i) for t, i in order], out
-
-    def value_pieces(g):
-        slot = lax.rem(g, SLOTS)
-        out = [None, None]
-
-        def piece(c, i, t):
-            x = dot_t(vbuf[slot, i, :, t * TILE : (t + 1) * TILE], p_ref[i, :, t * TILE : (t + 1) * TILE])
-            out[c] = x if out[c] is None else out[c] + x
-
-        order = [(c, c * SEQS // 2 + i, t) for i in range(SEQS // 2) for t in range(tiles) for c in range(2)]
-        return [functools.partial(piece, *o) for o in order], out
+        columns = [pl.ds(t, TILE) for t in range(0, cache, TILE)]
+        return jnp.concatenate([dot(qcat[group], kbuf[slot, :, :, c].reshape(SEQS * width, TILE)) for c in columns], 1)
+
+    def values(g):
+        slot, half = lax.rem(g, SLOTS), SEQS // 2
+        sums = [None, None]
+        for i in range(half):
+            for c in range(2):
+                x = dot_t(vbuf[slot, c * half + i], p_ref[c * half + i])
+                sums[c] = x if i == 0 else sums[c] + x
+        return sums
 
     def store_weights(s):
         e = jnp.exp((s - jnp.max(s, -1, keepdims=True)) * HEAD**-0.5)
@@ -152,9 +143,12 @@
         for i in range(SEQS):
             p_ref[i] = jnp.where(lax.rem(row, SEQS) == i, w, 0.0).astype(BF16)
 
-    def folded(sums):
+    def store_results(g, sums):
+        odd = lax.rem(g, 2)
         acc = jnp.where(vcol // SEQS == vrow // HEAD, sums[0] + sums[1], 0.0)
-        return dot_t(fold, acc.astype(BF16)).astype(BF16)
+        fold = jnp.where(lax.rem(fold_c, SEQS) + SEQS * odd == fold_r, 1.0, 0.0).astype(BF16)
+        other = jnp.where(res_r // SEQS == odd, 0.0, o_ref[...].astype(F32))
+        o_ref[...] = (other + dot_t(fold, acc.astype(BF16))).astype(BF16)
 
     def term1(b, k, to):
         return pltpu.make_async_remote_copy(
@@ -163,7 +157,7 @@
 
     def gather1(b, p):
         return pltpu.make_async_remote_copy(
-            h_own.at[b], h_in.at[b, p - 1], send2.at[b], recv2.at[b], device_id={axis: peer(p)}, device_id_type=MESH
+            b_own.at[b], b_in.at[b, p - 1], send2.at[b], recv2.at[b], device_id={axis: peer(p)}, device_id_type=MESH
         )
 
     def term2(b, p):
@@ -188,16 +182,17 @@
             all_of(landed, b, send1, recv1).wait_recv()
         for k in range(n - 1):
             h = h + landed[b, k].astype(F32)
-        h_own[b] = h.astype(BF16)
+        h = h.astype(BF16)
+        h_own[b] = h
+        b_own[b] = normed(h.astype(F32), gm[...].astype(F32)[None]).astype(BF16)
         for p in far_first:
             gather1(b, p).start()
 
     def mlp(b):
         with jax.named_scope("gather1_wait"):
-            all_of(h_in, b, send2, recv2).wait_recv()
-        gain = gm[...].astype(F32)[None]
+            all_of(b_in, b, send2, recv2).wait_recv()
         for j in range(n):
-            b_ref[j * SEQS : (j + 1) * SEQS, :] = normed((h_in[b, j - 1] if j else h_own[b]).astype(F32), gain)
+            b_ref[j * SEQS : (j + 1) * SEQS, :] = (b_in[b, j - 1] if j else b_own[b]).astype(F32)
         states = b_ref[...].astype(BF16)
         gate, up = dot(states, wg[...]), dot(states, wu[...])
         hidden = (gate * (1.0 / (1.0 + jnp.exp(-gate))) * up).astype(BF16)
@@ -220,10 +215,7 @@
 
     with jax.named_scope("k0_wait"):
         k_copy(0).wait()
-    todo, s = score_pieces(0)
-    for piece in todo:
-        piece()
-    store_weights(jnp.concatenate(s, 1))
+    store_weights(scores(0))
     o_ref[...] = jnp.zeros_like(o_ref)
     k_copy(SLOTS).start()
     with jax.named_scope("wo_wait"):
@@ -235,28 +227,35 @@
         terms[g // n, lax.rem(g, n)] = part.astype(BF16)
         term1(g // n, lax.rem(g, n), block_of(g)).start()
 
+    def send_pair(g):
+        part = dot(o_ref[...], wo[...])
+        send_term(g - 2, part[:SEQS])
+
+        @pl.when(lax.rem(g, n) == 0)
+        def _():
+            finish_h(0, part[SEQS:])
+
+        @pl.when(lax.rem(g, n) > 0)
+        def _():
+            send_term(g - 1, part[SEQS:])
+
     def body(g, carry):
         @pl.when(g == steps - SLOTS)
         def _():
             for c in third:
                 c.start()
+
+        @pl.when(jnp.logical_and(lax.rem(g, 2) == 0, g > 0))
+        def _():
+            send_pair(g)
 
         with jax.named_scope("kv_wait"):
             k_copy(g + 1).wait()
             v_copy(g).wait()
-        ks, s = score_pieces(g + 1)
-        vs, sums = value_pieces(g)
-        before = o_ref[...]
-        part = []
-        for j in range(len(vs)):
-            for piece in ks[2 * j : 2 * j + 2]:
-                piece()
-            vs[j]()
-            if j % 2:
-                part.append(dot(before, wo[:, j // 2 * TILE : (j // 2 + 1) * TILE]))
-        o_ref[...] = folded(sums)
-        store_weights(jnp.concatenate(s, 1))
-        part = jnp.concatenate(part, 1)[:SEQS]
+        s = scores(g + 1)
+        sums = values(g)
+        store_results(g, sums)
+        store_weights(s)
 
         @pl.when(g + 1 + SLOTS < steps)
         def _():
@@ -266,37 +265,39 @@
         def _():
             v_copy(g + SLOTS).start()
 
-        own_before = lax.rem(g, n) == 0
-
-        @pl.when(jnp.logical_not(own_before))
-        def _():
-            send_term(g - 1, part)
-
-        @pl.when(jnp.logical_and(own_before, g > 0))
-        def _():
-            finish_h(0, part)
-
         return carry
 
-    lax.fori_loop(0, steps - 1, body, 0)
-    g = steps - 1
+    lax.fori_loop(0, steps - 2, body, 0)
+    g = steps - 2
 
     @pl.when(me >= 0)
     def _():
-        send_term(g - 1, dot(o_ref[...], wo[...])[:SEQS])
-        with jax.named_scope("last_v_wait"):
+        send_pair(g)
+        with jax.named_scope("last_wait"):
             v_copy(g).wait()
 
     @pl.when(me < n)
     def _():
-        vs, sums = value_pieces(g)
-        for piece in vs:
-            piece()
-        o_ref[...] = folded(sums)
+        store_results(g, values(g))
 
     @pl.when(me > -1)
     def _():
-        finish_h(parts - 1, dot(o_ref[...], wo[...])[:SEQS])
+        send_term(g, dot(o_ref[...], wo[...])[:SEQS])
+        with jax.named_scope("last_wait"):
+            k_copy(g + 1).wait()
+            v_copy(g + 1).wait()
+
+    @pl.when(me < n + 1)
+    def _():
+        store_weights(scores(g + 1))
+
+    @pl.when(me > -2)
+    def _():
+        store_results(g + 1, values(g + 1))
+
+    @pl.when(me < n + 2)
+    def _():
+        finish_h(parts - 1, dot(o_ref[...], wo[...])[SEQS:])
 
     with jax.named_scope("third_wait"):
         for c in third:
@@ -322,7 +323,7 @@
     with jax.named_scope("send_wait"):
         for b in range(parts):
             all_of(terms, b, send1, recv1).wait_send()
-            all_of(h_in, b, send2, recv2).wait_send()
+            all_of(b_in, b, send2, recv2).wait_send()
             all_of(terms2, b, send3, recv3).wait_send()
             all_of(y_all, b, send4, recv4).wait_send()
 
@@ -367,9 +368,10 @@
                 pltpu.VMEM((SLOTS, SEQS, width, cache), BF16),
                 pltpu.VMEM((steps, rows, SEQS * width), BF16),
                 pltpu.VMEM((SEQS, rows, cache), BF16),
-                pltpu.VMEM((8, width), BF16),
+                pltpu.VMEM((2 * SEQS, width), BF16),
                 pltpu.VMEM((parts, n - 1, SEQS, d), BF16),
                 pltpu.VMEM((parts, n - 1, SEQS, d), BF16),
+                pltpu.VMEM((parts, SEQS, d), BF16),
                 pltpu.VMEM((parts, SEQS, d), BF16),
                 pltpu.VMEM((parts, n - 1, SEQS, d), BF16),
                 pltpu.VMEM((n * SEQS, d), F32),

time: 52.1 us -> 53.7 us (1.031); the launches traced: 52 us -> 52.7 us
  Pallas kernels: 51.2 us -> 52 us
    pallas_call x1, Pallas kernels: 51.2 us -> 52 us  [step(): pl.pallas_call(functools.partial(kernel, n, heads, 'tp'), out_shape=jax.S...]
where the time goes in v5:
time: 53.7 us; the launch traced here: 52.7 us
  Pallas kernels  52 us (97%)
  local copies, waits for them, and re-layouts  0.71 us (1%)
    pallas_call x1, Pallas kernels, step(): pl.pallas_call(functools.partial(kernel, n, heads, 'tp'), out_shape=jax.S...  52 us

profile of v5, /device:TPU:28, one launch (start us, length us, event | category | flops | bytes accessed | tf_op | source)
XLA Modules:
  0.0 52.7 jit_solution(7977849613876365584)
XLA Ops:
  0.0 52.0 %shard_map.109 = bf16[8,8,2048]{2,1,0:T(8,128)(2,1)S(1)} custom-call(bf16[8,8,2048]{2,1,0:T(8,128)(2,1)} %bitcast.11, bf16[16,4,256,1024]{3,2,1,0:T(8,128)(2,1)} %bitcast.9, bf16[16,4,256,1024]{3,2,1,0:T(8,128)(2,1)} %bitcast.10, bf16[2048]{0:T(1024)(128)(2,1)} %ga_hbm.1, bf16[2048,256]{1,0:T(8,128)(2,1)} %wq_hbm.1, bf16[256,2048]{1,0:T(8,128)(2,1)} %wo_hbm.1, ...), custom_call_target="tpu_custom_call" | custom-call | tf_op jit(solution)/shard_map/pallas_call | solution.py:352
  52.0 0.7 %copy.13 = bf16[64,2048]{1,0:T(8,128)(2,1)} copy(bf16[64,2048]{1,0:T(8,128)(2,1)S(1)} %bitcast.8) | data formatting | bytes 524288

commit v6 on v5

--- a/solution.py
+++ b/solution.py
@@ -121,6 +121,7 @@
     vcol = lax.broadcasted_iota(jnp.int32, (width, rows), 1)
     fold_r = lax.broadcasted_iota(jnp.int32, (2 * SEQS, rows), 0)
     fold_c = lax.broadcasted_iota(jnp.int32, (2 * SEQS, rows), 1)
+    tiles = cache // TILE
     res_r = lax.broadcasted_iota(jnp.int32, (2 * SEQS, width), 0)
 
     def scores(g):
@@ -136,6 +137,28 @@
                 x = dot_t(vbuf[slot, c * half + i], p_ref[c * half + i])
                 sums[c] = x if i == 0 else sums[c] + x
         return sums
+
+    def score_pieces(g):
+        slot, group = lax.rem(g, SLOTS), group_of(g)
+        out = [None] * tiles
+
+        def piece(t, i):
+            x = dot(qcat[group, :, i * width : (i + 1) * width], kbuf[slot, i, :, t * TILE : (t + 1) * TILE])
+            out[t] = x if out[t] is None else out[t] + x
+
+        order = [(t, i) for u in range(0, tiles, 2) for i in range(SEQS) for t in range(u, min(u + 2, tiles))]
+        return [functools.partial(piece, t, i) for t, i in order], out
+
+    def value_pieces(g):
+        slot = lax.rem(g, SLOTS)
+        out = [None, None]
+
+        def piece(c, i, t):
+            x = dot_t(vbuf[slot, i, :, t * TILE : (t + 1) * TILE], p_ref[i, :, t * TILE : (t + 1) * TILE])
+            out[c] = x if out[c] is None else out[c] + x
+
+        order = [(c, c * SEQS // 2 + i, t) for i in range(SEQS // 2) for t in range(tiles) for c in range(2)]
+        return [functools.partial(piece, *o) for o in order], out
 
     def store_weights(s):
         e = jnp.exp((s - jnp.max(s, -1, keepdims=True)) * HEAD**-0.5)
@@ -252,10 +275,13 @@
         with jax.named_scope("kv_wait"):
             k_copy(g + 1).wait()
             v_copy(g).wait()
-        s = scores(g + 1)
-        sums = values(g)
+        ks, s = score_pieces(g + 1)
+        vs, sums = value_pieces(g)
+        for j in range(len(vs)):
+            ks[j]()
+            vs[j]()
         store_results(g, sums)
-        store_weights(s)
+        store_weights(jnp.concatenate(s, 1))
 
         @pl.when(g + 1 + SLOTS < steps)
         def _():
@@ -267,13 +293,13 @@
 
         return carry
 
-    lax.fori_loop(0, steps - 2, body, 0)
-    g = steps - 2
+    lax.fori_loop(0, steps - 1, body, 0)
+    g = steps - 1
 
     @pl.when(me >= 0)
     def _():
-        send_pair(g)
-        with jax.named_scope("last_wait"):
+        send_term(g - 1, dot(o_ref[...], wo[...])[:SEQS])
+        with jax.named_scope("last_v_wait"):
             v_copy(g).wait()
 
     @pl.when(me < n)
@@ -281,21 +307,6 @@
         store_results(g, values(g))
 
     @pl.when(me > -1)
-    def _():
-        send_term(g, dot(o_ref[...], wo[...])[:SEQS])
-        with jax.named_scope("last_wait"):
-            k_copy(g + 1).wait()
-            v_copy(g + 1).wait()
-
-    @pl.when(me < n + 1)
-    def _():
-        store_weights(scores(g + 1))
-
-    @pl.when(me > -2)
-    def _():
-        store_results(g + 1, values(g + 1))
-
-    @pl.when(me < n + 2)
     def _():
         finish_h(parts - 1, dot(o_ref[...], wo[...])[SEQS:])
 

time: 53.7 us -> 54.5 us (1.015); the launches traced: 52.7 us -> 54.4 us
  Pallas kernels: 52 us -> 53.7 us
    pallas_call x1, Pallas kernels: 52 us -> 53.7 us  [step(): pl.pallas_call(functools.partial(kernel, n, heads, 'tp'), out_shape=jax.S...]
where the time goes in v6:
time: 54.5 us; the launch traced here: 54.4 us
  Pallas kernels  53.7 us (99%)
  local copies, waits for them, and re-layouts  0.71 us (1%)
    pallas_call x1, Pallas kernels, step(): pl.pallas_call(functools.partial(kernel, n, heads, 'tp'), out_shape=jax.S...  53.7 us

profile of v6, /device:TPU:28, one launch (start us, length us, event | category | flops | bytes accessed | tf_op | source)
XLA Modules:
  0.0 54.4 jit_solution(10827221473106495859)
XLA Ops:
  0.0 53.7 %shard_map.109 = bf16[8,8,2048]{2,1,0:T(8,128)(2,1)S(1)} custom-call(bf16[8,8,2048]{2,1,0:T(8,128)(2,1)} %bitcast.11, bf16[16,4,256,1024]{3,2,1,0:T(8,128)(2,1)} %bitcast.9, bf16[16,4,256,1024]{3,2,1,0:T(8,128)(2,1)} %bitcast.10, bf16[2048]{0:T(1024)(128)(2,1)} %ga_hbm.1, bf16[2048,256]{1,0:T(8,128)(2,1)} %wq_hbm.1, bf16[256,2048]{1,0:T(8,128)(2,1)} %wo_hbm.1, ...), custom_call_target="tpu_custom_call" | custom-call | tf_op jit(solution)/shard_map/pallas_call | solution.py:363
  53.7 0.7 %copy.13 = bf16[64,2048]{1,0:T(8,128)(2,1)} copy(bf16[64,2048]{1,0:T(8,128)(2,1)S(1)} %bitcast.8) | data formatting | bytes 524288

commit v7 on v3

--- a/solution.py
+++ b/solution.py
@@ -38,7 +38,7 @@
     x_hbm, k_hbm, v_hbm, ga_hbm, wq_hbm, wo_hbm, gm_hbm, wg_hbm, wu_hbm, wd_hbm, rope_hbm,
     y_ref,
     xs, ga, gm, rope, wq, wo, wg, wu, wd,
-    kbuf, vbuf, qcat, p_ref, o_ref, terms, landed, h_own, h_in, b_ref, own2, terms2, landed2, y_all,
+    kbuf, vbuf, qcat, p_ref, o_ref, terms, landed, h_own, b_own, b_in, b_ref, own2, terms2, landed2, y_all,
     k_sem, v_sem, w_sem, send1, recv1, send2, recv2, send3, recv3, send4, recv4,
 ):
     me = lax.axis_index(axis)
@@ -70,13 +70,13 @@
         pltpu.make_async_copy(ga_hbm, ga, w_sem.at[1]),
         pltpu.make_async_copy(wq_hbm, wq, w_sem.at[2]),
         pltpu.make_async_copy(rope_hbm, rope, w_sem.at[3]),
+        pltpu.make_async_copy(gm_hbm, gm, w_sem.at[8]),
     ]
     wo_copy = pltpu.make_async_copy(wo_hbm, wo, w_sem.at[4])
     third = [
         pltpu.make_async_copy(wg_hbm, wg, w_sem.at[5]),
         pltpu.make_async_copy(wu_hbm, wu, w_sem.at[6]),
         pltpu.make_async_copy(wd_hbm, wd, w_sem.at[7]),
-        pltpu.make_async_copy(gm_hbm, gm, w_sem.at[8]),
     ]
 
     for c in first:
@@ -163,7 +163,7 @@
 
     def gather1(b, p):
         return pltpu.make_async_remote_copy(
-            h_own.at[b], h_in.at[b, p - 1], send2.at[b], recv2.at[b], device_id={axis: peer(p)}, device_id_type=MESH
+            b_own.at[b], b_in.at[b, p - 1], send2.at[b], recv2.at[b], device_id={axis: peer(p)}, device_id_type=MESH
         )
 
     def term2(b, p):
@@ -188,16 +188,17 @@
             all_of(landed, b, send1, recv1).wait_recv()
         for k in range(n - 1):
             h = h + landed[b, k].astype(F32)
-        h_own[b] = h.astype(BF16)
+        h = h.astype(BF16)
+        h_own[b] = h
+        b_own[b] = normed(h.astype(F32), gm[...].astype(F32)[None]).astype(BF16)
         for p in far_first:
             gather1(b, p).start()
 
     def mlp(b):
         with jax.named_scope("gather1_wait"):
-            all_of(h_in, b, send2, recv2).wait_recv()
-        gain = gm[...].astype(F32)[None]
+            all_of(b_in, b, send2, recv2).wait_recv()
         for j in range(n):
-            b_ref[j * SEQS : (j + 1) * SEQS, :] = normed((h_in[b, j - 1] if j else h_own[b]).astype(F32), gain)
+            b_ref[j * SEQS : (j + 1) * SEQS, :] = (b_in[b, j - 1] if j else b_own[b]).astype(F32)
         states = b_ref[...].astype(BF16)
         gate, up = dot(states, wg[...]), dot(states, wu[...])
         hidden = (gate * (1.0 / (1.0 + jnp.exp(-gate))) * up).astype(BF16)
@@ -278,16 +279,36 @@
 
         return carry
 
-    lax.fori_loop(0, steps - 1, body, 0)
+    lax.fori_loop(0, steps - 2, body, 0)
     g = steps - 1
 
     @pl.when(me >= 0)
     def _():
+        with jax.named_scope("last_wait"):
+            v_copy(g - 1).wait()
+        vs, sums = value_pieces(g - 1)
+        part = dot(o_ref[...], wo[...])[:SEQS]
+        for piece in vs:
+            piece()
+        o_ref[...] = folded(sums)
+        send_term(g - 2, part)
+
+    @pl.when(me < n)
+    def _():
         send_term(g - 1, dot(o_ref[...], wo[...])[:SEQS])
+        with jax.named_scope("last_wait"):
+            k_copy(g).wait()
+
+    @pl.when(me < n + 1)
+    def _():
+        ks, s = score_pieces(g)
+        for piece in ks:
+            piece()
+        store_weights(jnp.concatenate(s, 1))
         with jax.named_scope("last_v_wait"):
             v_copy(g).wait()
 
-    @pl.when(me < n)
+    @pl.when(me > -2)
     def _():
         vs, sums = value_pieces(g)
         for piece in vs:
@@ -322,7 +343,7 @@
     with jax.named_scope("send_wait"):
         for b in range(parts):
             all_of(terms, b, send1, recv1).wait_send()
-            all_of(h_in, b, send2, recv2).wait_send()
+            all_of(b_in, b, send2, recv2).wait_send()
             all_of(terms2, b, send3, recv3).wait_send()
             all_of(y_all, b, send4, recv4).wait_send()
 
@@ -371,6 +392,7 @@
                 pltpu.VMEM((parts, n - 1, SEQS, d), BF16),
                 pltpu.VMEM((parts, n - 1, SEQS, d), BF16),
                 pltpu.VMEM((parts, SEQS, d), BF16),
+                pltpu.VMEM((parts, SEQS, d), BF16),
                 pltpu.VMEM((parts, n - 1, SEQS, d), BF16),
                 pltpu.VMEM((n * SEQS, d), F32),
                 pltpu.VMEM((parts, SEQS, d), F32),

time: 52.1 us -> 52.3 us (level)
  no operation moved by 1% of the time
where the time goes in v7:
time: 52.3 us
  Pallas kernels  51.6 us (99%)
  local copies, waits for them, and re-layouts  0.71 us (1%)
    pallas_call x1, Pallas kernels, step(): pl.pallas_call(functools.partial(kernel, n, heads, 'tp'), out_shape=jax.S...  51.6 us

profile of v7, /device:TPU:28, one launch (start us, length us, event | category | flops | bytes accessed | tf_op | source)
XLA Modules:
  0.0 52.3 jit_solution(5524679039451946318)
XLA Ops:
  0.0 51.6 %shard_map.109 = bf16[8,8,2048]{2,1,0:T(8,128)(2,1)S(1)} custom-call(bf16[8,8,2048]{2,1,0:T(8,128)(2,1)} %bitcast.11, bf16[16,4,256,1024]{3,2,1,0:T(8,128)(2,1)} %bitcast.9, bf16[16,4,256,1024]{3,2,1,0:T(8,128)(2,1)} %bitcast.10, bf16[2048]{0:T(1024)(128)(2,1)} %ga_hbm.1, bf16[2048,256]{1,0:T(8,128)(2,1)} %wq_hbm.1, bf16[256,2048]{1,0:T(8,128)(2,1)} %wo_hbm.1, ...), custom_call_target="tpu_custom_call" | custom-call | tf_op jit(solution)/shard_map/pallas_call | solution.py:372
  51.6 0.7 %copy.13 = bf16[64,2048]{1,0:T(8,128)(2,1)} copy(bf16[64,2048]{1,0:T(8,128)(2,1)S(1)} %bitcast.8) | data formatting | bytes 524288

commit v8 on v7

--- a/solution.py
+++ b/solution.py
@@ -158,7 +158,7 @@
 
     def term1(b, k, to):
         return pltpu.make_async_remote_copy(
-            terms.at[b, k], landed.at[b, k], send1.at[b], recv1.at[b], device_id={axis: to}, device_id_type=MESH
+            terms.at[b, k], landed.at[b, k], send1.at[b], recv1.at[b, k // (n - 2)], device_id={axis: to}, device_id_type=MESH
         )
 
     def gather1(b, p):
@@ -185,9 +185,15 @@
     def finish_h(b, own):
         h = xs[me].astype(F32)[b * SEQS : (b + 1) * SEQS] + own
         with jax.named_scope(f"term1_wait#b={b}"):
-            all_of(landed, b, send1, recv1).wait_recv()
-        for k in range(n - 1):
+            some = landed.at[b, pl.ds(0, n - 2)]
+            pltpu.make_async_remote_copy(
+                some, some, send1.at[b], recv1.at[b, 0], device_id={axis: me}, device_id_type=MESH
+            ).wait_recv()
+        for k in range(n - 2):
             h = h + landed[b, k].astype(F32)
+        with jax.named_scope(f"term1_last_wait#b={b}"):
+            term1(b, n - 2, me).wait_recv()
+        h = h + landed[b, n - 2].astype(F32)
         h = h.astype(BF16)
         h_own[b] = h
         b_own[b] = normed(h.astype(F32), gm[...].astype(F32)[None]).astype(BF16)
@@ -342,7 +348,7 @@
 
     with jax.named_scope("send_wait"):
         for b in range(parts):
-            all_of(terms, b, send1, recv1).wait_send()
+            all_of(terms, b, send1, send1).wait_send()
             all_of(b_in, b, send2, recv2).wait_send()
             all_of(terms2, b, send3, recv3).wait_send()
             all_of(y_all, b, send4, recv4).wait_send()
@@ -403,7 +409,8 @@
                 dma((SLOTS,)),
                 dma((9,)),
             ]
-            + [dma((parts,))] * 8,
+            + [dma((parts,)), dma((parts, 2))]
+            + [dma((parts,))] * 6,
             compiler_params=pltpu.CompilerParams(collective_id=0, has_side_effects=True, vmem_limit_bytes=VMEM_LIMIT),
         )(
             *(

time: 52.3 us -> 52.7 us (level)
  no operation moved by 1% of the time
where the time goes in v8:
time: 52.7 us; the launch traced here: 52.6 us
  Pallas kernels  51.9 us (98%)
  local copies, waits for them, and re-layouts  0.71 us (1%)
    pallas_call x1, Pallas kernels, step(): pl.pallas_call(functools.partial(kernel, n, heads, 'tp'), out_shape=jax.S...  51.9 us

profile of v8, /device:TPU:28, one launch (start us, length us, event | category | flops | bytes accessed | tf_op | source)
XLA Modules:
  0.0 52.6 jit_solution(12234012456113633771)
XLA Ops:
  0.0 51.9 %shard_map.109 = bf16[8,8,2048]{2,1,0:T(8,128)(2,1)S(1)} custom-call(bf16[8,8,2048]{2,1,0:T(8,128)(2,1)} %bitcast.11, bf16[16,4,256,1024]{3,2,1,0:T(8,128)(2,1)} %bitcast.9, bf16[16,4,256,1024]{3,2,1,0:T(8,128)(2,1)} %bitcast.10, bf16[2048]{0:T(1024)(128)(2,1)} %ga_hbm.1, bf16[2048,256]{1,0:T(8,128)(2,1)} %wq_hbm.1, bf16[256,2048]{1,0:T(8,128)(2,1)} %wo_hbm.1, ...), custom_call_target="tpu_custom_call" | custom-call | tf_op jit(solution)/shard_map/pallas_call | solution.py:378
  51.9 0.7 %copy.13 = bf16[64,2048]{1,0:T(8,128)(2,1)} copy(bf16[64,2048]{1,0:T(8,128)(2,1)S(1)} %bitcast.8) | data formatting | bytes 524288
